TPU v7x, 8 devices: a whole 2x2x1 slice. The times are simulated.
8 devices in a mesh: dp: 1 (over z), tp: 8 (over x, y, core).
Axes of the slice: x: 2, y: 2, z: 1, core: 2. Of those that a mesh axis runs over, the one named last changes fastest.
Arguments:
- x: bfloat16 [768, 12288], P(('dp', 'tp'))
- w_gate: bfloat16 [12288, 33792], P(None, 'tp')
- w_up: bfloat16 [12288, 33792], P(None, 'tp')
- w_down: bfloat16 [33792, 12288], P('tp')
Outputs:
- output: bfloat16 [768, 12288], P(('dp', 'tp'))
All inputs are finite; a program needn't handle non-finite values.
Results may differ from a plain program's by a relative error of at most 0.016.
Values are sent between devices in bfloat16 or wider.
A program may use at most 2 GiB of HBM per device.

v0:
```python
import jax
import jax.numpy as jnp
from jax import lax
from jax.sharding import PartitionSpec as P


def solution(mesh):
    def step(x, w_gate, w_up, w_down):
        rows = lax.all_gather(x, "tp", axis=0, tiled=True)
        gate = jnp.dot(rows, w_gate, preferred_element_type=jnp.float32)
        up = jnp.dot(rows, w_up, preferred_element_type=jnp.float32)
        hidden = (jax.nn.silu(gate) * up).astype(jnp.bfloat16)
        term = jnp.dot(hidden, w_down, preferred_element_type=jnp.float32).astype(jnp.bfloat16)
        return lax.psum_scatter(term, "tp", scatter_dimension=0, tiled=True)

    return jax.shard_map(
        step,
        mesh=mesh,
        in_specs=(P(("dp", "tp"), None), P(None, "tp"), P(None, "tp"), P("tp", None)),
        out_specs=P(("dp", "tp"), None),
        check_vma=False,
    )
```

profile of v0, /device:TPU:0, one launch (start us, length us, event | category | flops | bytes accessed | tf_op | source)
XLA Modules:
  0.0 508.4 jit_solution(10625605561355553487)
XLA Ops:
  6.5 0.0 all-gather.2.cloned.1.call-start
  6.5 0.7 all-gather.2.cloned.1.call-update
  7.3 0.0 reduce-scatter.2.cloned.1.call-start
  7.3 97.7 %all-gather.2.cloned.1.call-done = bf16[768,12288]{1,0:T(8,128)(2,1)} async-done(((bf16[96,12288]{1,0:T(8,128)(2,1)}), bf16[768,12288]{1,0:T(8,128)(2,1)}) %all-gather.2.cloned.1.call-update) | async-done | bytes 18874384 | tf_op jit(solution)/shard_map/all_gather | solution.py:9
  105.0 94.2 %fusion = f32[768,4224]{1,0:T(8,128)} fusion(bf16[768,12288]{1,0:T(8,128)(2,1)} %all-gather.2.cloned.1.call-done, bf16[12288,4224]{1,0:T(8,128)(2,1)} %param.5), kind=kOutput, calls=%fused_computation.2 | convolution fusion | flops 79725330432 | bytes 135659520 | tf_op jit(solution)/shard_map/dot_general | solution.py:10
  199.2 94.6 %multiply_convert_fusion = bf16[768,4224]{1,0:T(8,128)(2,1)S(1)} fusion(f32[768,4224]{1,0:T(8,128)} %fusion, bf16[768,12288]{1,0:T(8,128)(2,1)} %all-gather.2.cloned.1.call-done, bf16[12288,4224]{1,0:T(8,128)(2,1)} %param.6), kind=kOutput, calls=%fused_computation.1 | convolution fusion | flops 79744794624 | bytes 142147584 | tf_op jit(solution)/shard_map/dot_general | solution.py:11
  293.8 90.5 %convolution_convert_fusion = bf16[768,12288]{1,0:T(8,128)(2,1)} fusion(bf16[768,4224]{1,0:T(8,128)(2,1)S(1)} %multiply_convert_fusion, bf16[4224,12288]{1,0:T(8,128)(2,1)} %param.7), kind=kOutput, calls=%fused_computation | convolution fusion | flops 79734767616 | bytes 129171456 | tf_op jit(solution)/shard_map/dot_general | solution.py:13
  384.4 0.0 reduce-scatter.2.cloned.1.call-update
  384.4 117.2 %reduce-scatter.2.cloned.1.call-done = bf16[96,12288]{1,0:T(8,128)(2,1)} async-done(((bf16[768,12288]{1,0:T(8,128)(2,1)}), bf16[96,12288]{1,0:T(8,128)(2,1)}) %reduce-scatter.2.cloned.1.call-update) | async-done | bytes 2359312 | tf_op jit(solution)/shard_map/reduce_scatter | solution.py:14
Async XLA Ops:
  6.5 98.4 %all-gather.2.cloned.1.call-start = ((), (), s32[]{:S(2)}) async-start(), calls=%async_computation.1 | async-start | bytes 21233664 | tf_op jit(solution)/shard_map/all_gather | solution.py:9
  7.3 494.3 %reduce-scatter.2.cloned.1.call-start = ((), (), s32[]{:S(2)}) async-start(), calls=%async_computation.2 | async-start | bytes 21233664 | tf_op jit(solution)/shard_map/reduce_scatter | solution.py:14
Sparse Core Ops, SparseCore 0:
  9.1 95.7 all-gather.1
  384.5 117.0 reduce-scatter.1
where the time goes:
time: 509 us; the launch traced here: 508 us
  matrix products  279 us (55%)
  waiting for transfers between devices  216 us (42%)
  between operations  13.4 us (3%)
    reduce_scatter x1, waiting for transfers between devices, step(): return lax.psum_scatter(term, 'tp', scatter_dimension=0, tiled=True)  117 us
    all_gather x1, waiting for transfers between devices, step(): rows = lax.all_gather(x, 'tp', axis=0, tiled=True)  97.7 us
    dot_general x1, matrix products, step(): up = jnp.dot(rows, w_up, preferred_element_type=jnp.float32)  94.6 us
    dot_general x1, matrix products, step(): gate = jnp.dot(rows, w_gate, preferred_element_type=jnp.float32)  94.2 us
    dot_general x1, matrix products, step(): jnp.dot(hidden, w_down, preferred_element_type=jnp.float32)  90.5 us
  transfers between devices with their start and end apart: 2, of which 2 were waited for; matrix products, arithmetic and copies ran while one was open for 0% of the time, Pallas kernels for 0%

commit v1 on v0

v1 whole, which is shorter than its diff:
```python
import jax
import jax.numpy as jnp
from jax import lax
from jax.experimental import pallas as pl
from jax.experimental.pallas import tpu as pltpu
from jax.sharding import PartitionSpec as P

BF, F32 = jnp.bfloat16, jnp.float32
KC = 768
NB = 1408
NC = 512
VMEM = 67_000_000

SENDS = ((0, 1, 0), (0, 2, 1), (0, 4, 2), (2, 3, 0), (1, 5, 2), (2, 6, 2), (3, 7, 2))


def neighbours():
    me = lax.axis_index("tp")
    core, y, x = me % 2, (me // 2) % 2, me // 4
    over_x, over_y = me + 4 * (1 - 2 * x), me + 2 * (1 - 2 * y)
    a = over_x * (1 - core) + over_y * core
    b = over_x * core + over_y * (1 - core)
    return a, b, me + 1 - 2 * core


def greet(others):
    barrier = pltpu.get_barrier_semaphore()
    for other in others:
        pl.semaphore_signal(barrier, inc=1, device_id={"tp": other}, device_id_type=pl.DeviceIdType.MESH)
    pl.semaphore_wait(barrier, len(others))


def gather_up(x_ref, wg_ref, wu_ref, h_ref, xg, acc, wbuf, hbuf, lsem, ssem, rsem, wsem, hsem):
    rows = x_ref.shape[0]
    nk, nb, slots = xg.shape[0], acc.shape[0], wbuf.shape[0]
    total = nk * nb
    others = neighbours()

    def local(c):
        k0 = pl.multiple_of(c * KC, KC)
        return pltpu.make_async_copy(x_ref.at[:, pl.ds(k0, KC)], xg.at[c, pl.ds(0, rows)], lsem.at[c])

    def remote(kind, c):
        src, dst, to = SENDS[kind]
        return pltpu.make_async_remote_copy(
            src_ref=xg.at[c, pl.ds(src * rows, rows)],
            dst_ref=xg.at[c, pl.ds(dst * rows, rows)],
            send_sem=ssem.at[kind, c],
            recv_sem=rsem.at[kind, c],
            device_id={"tp": others[to]},
            device_id_type=pl.DeviceIdType.MESH,
        )

    def weights(s):
        k0, n0 = pl.multiple_of((s // nb) * KC, KC), pl.multiple_of((s % nb) * NB, 128)
        slot = s % slots
        return [
            pltpu.make_async_copy(
                w.at[pl.ds(k0, KC), pl.ds(n0, NB)], wbuf.at[slot, :, pl.ds(i * NB, NB)], wsem.at[slot, i]
            )
            for i, w in enumerate((wg_ref, wu_ref))
        ]

    def start(copies):
        for copy in copies:
            copy.start()

    def wait(copies):
        for copy in copies:
            copy.wait()

    def own(c):
        local(c).wait()
        for kind in (0, 1, 2):
            remote(kind, c).start()

    def pass_on(c):
        remote(1, c).wait_recv()
        remote(3, c).start()
        remote(5, c).start()
        remote(0, c).wait_recv()
        remote(4, c).start()

    def pass_far(c):
        remote(3, c).wait_recv()
        remote(6, c).start()

    def ready(c):
        for kind in (2, 4, 5, 6):
            remote(kind, c).wait_recv()

    local(0).start()
    start(weights(0))

    @pl.loop(1, nk)
    def _(c):
        local(c).start()

    for s in range(1, slots - 1):
        start(weights(s))
    greet(others)
    own(0)

    @pl.loop(0, nb)
    def _(n):
        @pl.loop(0, acc.shape[1] // 32)
        def _(r):
            acc[n, pl.ds(pl.multiple_of(r * 32, 32), 32), :] = jnp.zeros((32, 2 * NB), F32)

    pass_on(0)
    own(1)
    pass_far(0)

    def dot(c, s, n):
        acc[n] += jnp.dot(xg[c], wbuf[s % slots], preferred_element_type=F32)

    @pl.loop(0, total - nb)
    def _(s):
        c, n = s // nb, s % nb

        @pl.when(n == 0)
        def _():
            ready(c)

            @pl.when(c + 2 < nk)
            def _():
                own(c + 2)

        @pl.when(n == 1)
        def _():
            @pl.when(c == 0)
            def _():
                pass_on(1)

            @pl.when(c > 0)
            def _():
                pass_far(c + 1)

        @pl.when(n == 2)
        def _():
            @pl.when(c == 0)
            def _():
                pass_far(1)

            @pl.when(c + 2 < nk)
            def _():
                pass_on(c + 2)

        @pl.when(s + slots - 1 < total)
        def _():
            start(weights(s + slots - 1))

        wait(weights(s))
        dot(c, s, n)

    def put(n):
        return pltpu.make_async_copy(hbuf.at[n % 2], h_ref.at[:, pl.ds(n * NB, NB)], hsem.at[n % 2])

    def hide(n):
        for r in range(0, acc.shape[1], 16):
            gate, up = acc[n, r : r + 16, :NB], acc[n, r : r + 16, NB:]
            hbuf[n % 2, r : r + 16] = (jax.nn.silu(gate) * up).astype(BF)

    ready(nk - 1)
    for n in range(nb):
        s = total - nb + n
        if s + slots - 1 < total:
            start(weights(s + slots - 1))
        wait(weights(s))
        if n >= 3:
            put(n - 3).wait()
        if n >= 1:
            hide(n - 1)
        dot(nk - 1, s, n)
        if n >= 1:
            put(n - 1).start()
    if nb >= 3:
        put(nb - 3).wait()
    hide(nb - 1)
    put(nb - 1).start()
    put(nb - 2).wait()
    put(nb - 1).wait()

    @pl.loop(0, nk)
    def _(c):
        for kind in range(len(SENDS)):
            remote(kind, c).wait_send()


LAG = (2, 5, 8)
FREE = 8


def down_scatter(
    h_ref, wd_ref, y_ref, hid, wbuf, own, kept, part, yout, out_p, in_p, out_a, in_a, out_b, in_b,
    hsem, wsem, ysem, sems_p, sems_a, sems_b,
):
    rows = y_ref.shape[0]
    slots = wbuf.shape[0]
    count = y_ref.shape[1] // NC
    others = neighbours()

    def weights(i):
        n0 = pl.multiple_of(i * NC, NC)
        return pltpu.make_async_copy(wd_ref.at[:, pl.ds(n0, NC)], wbuf.at[i % slots], wsem.at[i % slots])

    def remote(i, out, into, sems, to):
        return pltpu.make_async_remote_copy(
            src_ref=out.at[i % 4],
            dst_ref=into.at[i + FREE],
            send_sem=sems.at[0, i],
            recv_sem=sems.at[1, i],
            device_id={"tp": others[to]},
            device_id_type=pl.DeviceIdType.MESH,
        )

    def to_p(i):
        return remote(i, out_p, in_p, sems_p, 2)

    def to_a(i):
        return remote(i, out_a, in_a, sems_a, 0)

    def to_b(i):
        return remote(i, out_b, in_b, sems_b, 1)

    def result(i):
        n0 = pl.multiple_of(i * NC, NC)
        return pltpu.make_async_copy(yout.at[i % 4], y_ref.at[:, pl.ds(n0, NC)], ysem.at[i % 4])

    def pair_sum(i):
        there = in_p[i + FREE]
        mine, slot = own.at[(i + FREE) % 4], (i + FREE) % 4
        out = out_a.at[slot]
        kept[(i + FREE) % 8, :rows] = mine[:rows] + there[:rows].astype(F32)
        kept[(i + FREE) % 8, rows:] = mine[2 * rows : 3 * rows] + there[2 * rows : 3 * rows].astype(F32)
        out[:rows] = (mine[rows : 2 * rows] + there[rows : 2 * rows].astype(F32)).astype(BF)
        out[rows:] = (mine[3 * rows :] + there[3 * rows :].astype(F32)).astype(BF)

    def next_sum(i):
        there = in_a[i + FREE]
        slot = (i + FREE) % 8
        part[slot] = kept[slot, :rows] + there[:rows].astype(F32)
        out_b[(i + FREE) % 4] = (kept[slot, rows:] + there[rows:].astype(F32)).astype(BF)

    def last_sum(i):
        yout[(i + FREE) % 4] = (part[(i + FREE) % 8] + in_b[i + FREE].astype(F32)).astype(BF)

    whole = pltpu.make_async_copy(h_ref, hid, hsem)
    whole.start()
    for i in range(slots - 1):
        weights(i).start()
    greet(others)
    whole.wait()

    @pl.loop(0, count)
    def _(i):
        @pl.when(i + slots - 1 < count)
        def _():
            weights(i + slots - 1).start()

        weights(i).wait()

        @pl.when(i >= 4)
        def _():
            to_p(i - 4).wait_send()

        @pl.when(i >= LAG[0])
        def _():
            to_p(i - LAG[0]).wait_recv()

        @pl.when(i >= LAG[0] + 4)
        def _():
            to_a(i - LAG[0] - 4).wait_send()

        @pl.when(i >= LAG[1])
        def _():
            to_a(i - LAG[1]).wait_recv()

        @pl.when(i >= LAG[1] + 4)
        def _():
            to_b(i - LAG[1] - 4).wait_send()

        @pl.when(i >= LAG[2])
        def _():
            to_b(i - LAG[2]).wait_recv()

        @pl.when(i >= LAG[2] + 4)
        def _():
            result(i - LAG[2] - 4).wait()

        last_sum(i - LAG[2])
        next_sum(i - LAG[1])
        pair_sum(i - LAG[0])
        term = jnp.dot(hid[...], wbuf[i % slots], preferred_element_type=F32)
        out_p[i % 4] = term[4 * rows :].astype(BF)
        own[i % 4] = term[: 4 * rows]

        @pl.when(i >= LAG[1])
        def _():
            to_b(i - LAG[1]).start()

        @pl.when(i >= LAG[0])
        def _():
            to_a(i - LAG[0]).start()

        @pl.when(i >= LAG[2])
        def _():
            result(i - LAG[2]).start()

        to_p(i).start()

    for i in range(count, count + LAG[2]):
        if i - LAG[0] < count:
            to_p(i - LAG[0]).wait_recv()
            to_a(i - LAG[0] - 4).wait_send()
            pair_sum(i - LAG[0])
            to_a(i - LAG[0]).start()
        if i - LAG[1] < count:
            to_a(i - LAG[1]).wait_recv()
            to_b(i - LAG[1] - 4).wait_send()
            next_sum(i - LAG[1])
            to_b(i - LAG[1]).start()
        to_b(i - LAG[2]).wait_recv()
        result(i - LAG[2] - 4).wait()
        last_sum(i - LAG[2])
        result(i - LAG[2]).start()
    for i in range(count - 4, count):
        to_p(i).wait_send()
        to_a(i).wait_send()
        to_b(i).wait_send()
        result(i).wait()


def solution(mesh):
    def step(x, w_gate, w_up, w_down):
        (rows, width), units = x.shape, w_gate.shape[1]
        tokens = rows * mesh.shape["tp"]
        nk, nb, count = width // KC, units // NB, width // NC
        dma = pltpu.SemaphoreType.DMA
        anywhere = pl.BlockSpec(memory_space=pl.ANY)
        h = pl.pallas_call(
            gather_up,
            out_shape=jax.ShapeDtypeStruct((tokens, units), BF),
            in_specs=[anywhere] * 3,
            out_specs=anywhere,
            scratch_shapes=[
                pltpu.VMEM((nk, tokens, KC), BF),
                pltpu.VMEM((nb, tokens, 2 * NB), F32),
                pltpu.VMEM((2, KC, 2 * NB), BF),
                pltpu.VMEM((2, tokens, NB), BF),
                dma((nk,)),
                dma((len(SENDS), nk)),
                dma((len(SENDS), nk)),
                dma((2, 2)),
                dma((2,)),
            ],
            compiler_params=pltpu.CompilerParams(collective_id=0, has_side_effects=True, vmem_limit_bytes=VMEM),
            name="gather_up",
        )(x, w_gate, w_up)
        return pl.pallas_call(
            down_scatter,
            out_shape=jax.ShapeDtypeStruct((rows, width), BF),
            in_specs=[anywhere] * 2,
            out_specs=anywhere,
            scratch_shapes=[
                pltpu.VMEM((tokens, units), BF),
                pltpu.VMEM((3, units, NC), BF),
                pltpu.VMEM((4, 4 * rows, NC), F32),
                pltpu.VMEM((8, 2 * rows, NC), F32),
                pltpu.VMEM((8, rows, NC), F32),
                pltpu.VMEM((4, rows, NC), BF),
                pltpu.VMEM((4, 4 * rows, NC), BF),
                pltpu.VMEM((count + FREE, 4 * rows, NC), BF),
                pltpu.VMEM((4, 2 * rows, NC), BF),
                pltpu.VMEM((count + FREE, 2 * rows, NC), BF),
                pltpu.VMEM((4, rows, NC), BF),
                pltpu.VMEM((count + FREE, rows, NC), BF),
                dma,
                dma((3,)),
                dma((4,)),
                dma((2, count)),
                dma((2, count)),
                dma((2, count)),
            ],
            compiler_params=pltpu.CompilerParams(collective_id=1, has_side_effects=True, vmem_limit_bytes=VMEM),
            name="down_scatter",
        )(h, w_down)

    return jax.shard_map(
        step,
        mesh=mesh,
        in_specs=(P(("dp", "tp"), None), P(None, "tp"), P(None, "tp"), P("tp", None)),
        out_specs=P(("dp", "tp"), None),
        check_vma=False,
    )
```

time: 509 us -> 312 us (0.61)
  Pallas kernels: 0 us -> 309 us
  matrix products: 279 us -> 0 us
  waiting for transfers between devices: 216 us -> 0 us
  between operations: 13.4 us -> 0.02 us
    pallas_call x0 -> x2, Pallas kernels: none -> 309 us  [the longest x1 195 us: step(): pl.pallas_call(gather_up, out_shape=jax.ShapeDtypeStruct((tokens, units),...]
    dot_general x3 -> x0, matrix products: 279 us -> none  [the longest x1 94.6 us: step(): up = jnp.dot(rows, w_up, preferred_element_type=jnp.float32)]
    reduce_scatter x1 -> x0, waiting for transfers between devices: 117 us -> none  [step(): return lax.psum_scatter(term, 'tp', scatter_dimension=0, tiled=True)]
    all_gather x1 -> x0, waiting for transfers between devices: 97.7 us -> none  [step(): rows = lax.all_gather(x, 'tp', axis=0, tiled=True)]
  transfers between devices with their start and end apart: 2 -> 0, of which waited for: 2 -> 0; matrix products, arithmetic and copies ran while one was open for 0% -> 0% of each run, Pallas kernels for 0% -> 0%
where the time goes in v1:
time: 312 us
  Pallas kernels  309 us (99%)
  local copies, waits for them, and re-layouts  3.22 us (1%)
    pallas_call x1, Pallas kernels, step(): pl.pallas_call(gather_up, out_shape=jax.ShapeDtypeStruct((tokens, units),...  195 us
    pallas_call x1, Pallas kernels, step(): pl.pallas_call(down_scatter, out_shape=jax.ShapeDtypeStruct((rows, width)...  113 us

profile of v1, /device:TPU:0, one launch (start us, length us, event | category | flops | bytes accessed | tf_op | source)
XLA Modules:
  0.0 311.8 jit_solution(1947729369794235440)
XLA Ops:
  0.0 195.3 %gather_up.1.h_ref = bf16[768,4224]{1,0:T(8,128)(2,1)} custom-call(bf16[96,12288]{1,0:T(8,128)(2,1)} %x_ref.1, bf16[12288,4224]{1,0:T(8,128)(2,1)} %wg_ref.1, bf16[12288,4224]{1,0:T(8,128)(2,1)} %wu_ref.1), custom_call_target="tpu_custom_call" | custom-call | tf_op jit(solution)/shard_map/gather_up/pallas_call | solution.py:341
  195.3 113.3 %down_scatter.1 = bf16[96,12288]{1,0:T(8,128)(2,1)} custom-call(bf16[768,4224]{1,0:T(8,128)(2,1)} %gather_up.1.h_ref, bf16[4224,12288]{1,0:T(8,128)(2,1)} %wd_ref.1), custom_call_target="tpu_custom_call" | custom-call | tf_op jit(solution)/shard_map/down_scatter/pallas_call | solution.py:360
  308.6 3.2 %copy.6 = bf16[96,12288]{1,0:T(8,128)(2,1)} copy(bf16[96,12288]{1,0:T(8,128)(2,1)} %down_scatter.1) | data formatting | bytes 4718592

commit v2 on v1

--- a/solution.py
+++ b/solution.py
@@ -6,8 +6,9 @@
 from jax.sharding import PartitionSpec as P
 
 BF, F32 = jnp.bfloat16, jnp.float32
-KC = 768
+KC = 1024
 NB = 1408
+PIECES = 4
 NC = 512
 VMEM = 67_000_000
 
@@ -30,7 +31,7 @@
     pl.semaphore_wait(barrier, len(others))
 
 
-def gather_up(x_ref, wg_ref, wu_ref, h_ref, xg, acc, wbuf, hbuf, lsem, ssem, rsem, wsem, hsem):
+def gather_up(x_ref, wg_ref, wu_ref, h_ref, xg, acc, wbuf, lsem, ssem, rsem, fssem, frsem, wsem, hsem):
     rows = x_ref.shape[0]
     nk, nb, slots = xg.shape[0], acc.shape[0], wbuf.shape[0]
     total = nk * nb
@@ -51,6 +52,18 @@
             device_id_type=pl.DeviceIdType.MESH,
         )
 
+    def first(kind, piece):
+        src, dst, to = SENDS[kind]
+        columns = pl.ds(piece * (KC // PIECES), KC // PIECES)
+        return pltpu.make_async_remote_copy(
+            src_ref=xg.at[0, pl.ds(src * rows, rows), columns],
+            dst_ref=xg.at[0, pl.ds(dst * rows, rows), columns],
+            send_sem=fssem.at[kind, piece],
+            recv_sem=frsem.at[kind, piece],
+            device_id={"tp": others[to]},
+            device_id_type=pl.DeviceIdType.MESH,
+        )
+
     def weights(s):
         k0, n0 = pl.multiple_of((s // nb) * KC, KC), pl.multiple_of((s % nb) * NB, 128)
         slot = s % slots
@@ -99,7 +112,10 @@
     for s in range(1, slots - 1):
         start(weights(s))
     greet(others)
-    own(0)
+    local(0).wait()
+    for piece in range(PIECES):
+        for kind in (0, 1, 2):
+            first(kind, piece).start()
 
     @pl.loop(0, nb)
     def _(n):
@@ -107,9 +123,20 @@
         def _(r):
             acc[n, pl.ds(pl.multiple_of(r * 32, 32), 32), :] = jnp.zeros((32, 2 * NB), F32)
 
-    pass_on(0)
-    own(1)
-    pass_far(0)
+    for piece in range(PIECES):
+        first(1, piece).wait_recv()
+        first(3, piece).start()
+        first(5, piece).start()
+        first(0, piece).wait_recv()
+        first(4, piece).start()
+    for piece in range(PIECES):
+        if piece == PIECES - 1:
+            own(1)
+        first(3, piece).wait_recv()
+        first(6, piece).start()
+    for piece in range(PIECES):
+        for kind in (2, 4, 5, 6):
+            first(kind, piece).wait_recv()
 
     def dot(c, s, n):
         acc[n] += jnp.dot(xg[c], wbuf[s % slots], preferred_element_type=F32)
@@ -120,7 +147,9 @@
 
         @pl.when(n == 0)
         def _():
-            ready(c)
+            @pl.when(c > 0)
+            def _():
+                ready(c)
 
             @pl.when(c + 2 < nk)
             def _():
@@ -154,12 +183,28 @@
         dot(c, s, n)
 
     def put(n):
-        return pltpu.make_async_copy(hbuf.at[n % 2], h_ref.at[:, pl.ds(n * NB, NB)], hsem.at[n % 2])
+        return [
+            pltpu.make_async_copy(xg.at[2 * n], h_ref.at[:, pl.ds(n * NB, KC)], hsem.at[n, 0]),
+            pltpu.make_async_copy(
+                xg.at[2 * n + 1, :, pl.ds(0, NB - KC)], h_ref.at[:, pl.ds(n * NB + KC, NB - KC)], hsem.at[n, 1]
+            ),
+        ]
 
     def hide(n):
         for r in range(0, acc.shape[1], 16):
             gate, up = acc[n, r : r + 16, :NB], acc[n, r : r + 16, NB:]
-            hbuf[n % 2, r : r + 16] = (jax.nn.silu(gate) * up).astype(BF)
+            hidden = (jax.nn.silu(gate) * up).astype(BF)
+            xg[2 * n, r : r + 16] = hidden[:, :KC]
+            xg[2 * n + 1, r : r + 16, : NB - KC] = hidden[:, KC:]
+
+    for piece in range(PIECES):
+        for kind in range(len(SENDS)):
+            first(kind, piece).wait_send()
+
+    @pl.loop(1, nk)
+    def _(c):
+        for kind in range(len(SENDS)):
+            remote(kind, c).wait_send()
 
     ready(nk - 1)
     for n in range(nb):
@@ -167,27 +212,18 @@
         if s + slots - 1 < total:
             start(weights(s + slots - 1))
         wait(weights(s))
-        if n >= 3:
-            put(n - 3).wait()
         if n >= 1:
             hide(n - 1)
         dot(nk - 1, s, n)
         if n >= 1:
-            put(n - 1).start()
-    if nb >= 3:
-        put(nb - 3).wait()
+            start(put(n - 1))
     hide(nb - 1)
-    put(nb - 1).start()
-    put(nb - 2).wait()
-    put(nb - 1).wait()
-
-    @pl.loop(0, nk)
-    def _(c):
-        for kind in range(len(SENDS)):
-            remote(kind, c).wait_send()
-
-
-LAG = (2, 5, 8)
+    start(put(nb - 1))
+    for n in range(nb):
+        wait(put(n))
+
+
+LAG = (1, 3, 5)
 FREE = 8
 
 
@@ -252,8 +288,7 @@
     greet(others)
     whole.wait()
 
-    @pl.loop(0, count)
-    def _(i):
+    def waits(i):
         @pl.when(i + slots - 1 < count)
         def _():
             weights(i + slots - 1).start()
@@ -288,26 +323,31 @@
         def _():
             result(i - LAG[2] - 4).wait()
 
+    def compute(i, summed, passed):
         last_sum(i - LAG[2])
         next_sum(i - LAG[1])
         pair_sum(i - LAG[0])
-        term = jnp.dot(hid[...], wbuf[i % slots], preferred_element_type=F32)
-        out_p[i % 4] = term[4 * rows :].astype(BF)
-        own[i % 4] = term[: 4 * rows]
-
-        @pl.when(i >= LAG[1])
-        def _():
+        w = wbuf.at[i % slots]
+        out_p[i % 4] = jnp.dot(hid[4 * rows :], w[...], preferred_element_type=F32).astype(BF)
+        if passed:
             to_b(i - LAG[1]).start()
-
-        @pl.when(i >= LAG[0])
-        def _():
+        if summed:
             to_a(i - LAG[0]).start()
+        to_p(i).start()
+        own[i % 4] = jnp.dot(hid[: 4 * rows], w[...], preferred_element_type=F32)
+
+    for i in range(LAG[1]):
+        waits(i)
+        compute(i, i >= LAG[0], False)
+
+    @pl.loop(LAG[1], count)
+    def _(i):
+        waits(i)
+        compute(i, True, True)
 
         @pl.when(i >= LAG[2])
         def _():
             result(i - LAG[2]).start()
-
-        to_p(i).start()
 
     for i in range(count, count + LAG[2]):
         if i - LAG[0] < count:
@@ -347,12 +387,13 @@
                 pltpu.VMEM((nk, tokens, KC), BF),
                 pltpu.VMEM((nb, tokens, 2 * NB), F32),
                 pltpu.VMEM((2, KC, 2 * NB), BF),
-                pltpu.VMEM((2, tokens, NB), BF),
                 dma((nk,)),
                 dma((len(SENDS), nk)),
                 dma((len(SENDS), nk)),
+                dma((len(SENDS), PIECES)),
+                dma((len(SENDS), PIECES)),
                 dma((2, 2)),
-                dma((2,)),
+                dma((nb, 2)),
             ],
             compiler_params=pltpu.CompilerParams(collective_id=0, has_side_effects=True, vmem_limit_bytes=VMEM),
             name="gather_up",

time: 312 us -> 306 us (0.981)
  Pallas kernels: 309 us -> 303 us
    pallas_call x1, Pallas kernels: 113 us -> 110 us  [step(): pl.pallas_call(down_scatter, out_shape=jax.ShapeDtypeStruct((rows, width)...]
where the time goes in v2:
time: 306 us
  Pallas kernels  303 us (99%)
  local copies, waits for them, and re-layouts  3.22 us (1%)
    pallas_call x1, Pallas kernels, step(): pl.pallas_call(gather_up, out_shape=jax.ShapeDtypeStruct((tokens, units),...  193 us
    pallas_call x1, Pallas kernels, step(): pl.pallas_call(down_scatter, out_shape=jax.ShapeDtypeStruct((rows, width)...  110 us

profile of v2, /device:TPU:0, one launch (start us, length us, event | category | flops | bytes accessed | tf_op | source)
XLA Modules:
  0.0 306.3 jit_solution(9358514757571465906)
XLA Ops:
  0.0 192.9 %gather_up.1.h_ref = bf16[768,4224]{1,0:T(8,128)(2,1)} custom-call(bf16[96,12288]{1,0:T(8,128)(2,1)} %x_ref.1, bf16[12288,4224]{1,0:T(8,128)(2,1)} %wg_ref.1, bf16[12288,4224]{1,0:T(8,128)(2,1)} %wu_ref.1), custom_call_target="tpu_custom_call" | custom-call | tf_op jit(solution)/shard_map/gather_up/pallas_call | solution.py:381
  192.9 110.1 %down_scatter.1 = bf16[96,12288]{1,0:T(8,128)(2,1)} custom-call(bf16[768,4224]{1,0:T(8,128)(2,1)} %gather_up.1.h_ref, bf16[4224,12288]{1,0:T(8,128)(2,1)} %wd_ref.1), custom_call_target="tpu_custom_call" | custom-call | tf_op jit(solution)/shard_map/down_scatter/pallas_call | solution.py:401
  303.0 3.2 %copy.6 = bf16[96,12288]{1,0:T(8,128)(2,1)} copy(bf16[96,12288]{1,0:T(8,128)(2,1)} %down_scatter.1) | data formatting | bytes 4718592
